TPU v7x, 32 devices: a whole 2x2x4 slice. The times are simulated.
32 devices in a mesh: row: 8 (over y, x, core), col: 4 (over z).
Axes of the slice: x: 2, y: 2, z: 4, core: 2. Of those that a mesh axis runs over, the one named last changes fastest.
Arguments:
- rotation: bfloat16 [8192, 8192], P('row', 'col'), may hold values from -0.0625 to 0.0625
- gradient: bfloat16 [8192, 8192], P('row', 'col'), may hold values from -0.0625 to 0.0625
Outputs:
- updated: float32 [8192, 2048], P('row', 'col')
- column_norms: float32 [2048], P('col')
All inputs are finite; a program needn't handle non-finite values.
Results may differ from a plain program's by a relative error of at most 0.01.
Values may be sent and summed in bfloat16 or wider, within the bound.
A program may use at most 128 MiB of HBM per device.

v0:
```python
import functools

import jax
import jax.numpy as jnp
from jax import lax
from jax.experimental import pallas as pl
from jax.experimental.pallas import tpu as pltpu
from jax.sharding import PartitionSpec as P

SLAB = 2048
PIECES = 4
TILE = 256
MESH = pl.DeviceIdType.MESH
NT = (((1,), (1,)), ((), ()))
UP, DOWN = 0, 1


def split(items, groups):
    size = -(-len(items) // groups)
    return [items[g * size : (g + 1) * size] for g in range(groups)]


def kernel(
    n_row, n_col,
    rot_hbm, grad_hbm, cols_hbm,
    out_ref, norm_ref,
    rot, grad, base, v, zp, zf, rbuf, y, zsend, zrecv, upd, fin, nrm, nrecv,
    load_sem, core_send, core_recv, rs_send, rs_recv, ag_send, ag_recv,
    up_send, up_recv, vg_send, vg_recv, fin_send, fin_recv, n_send, n_recv, local_sem,
):
    levels = n_row.bit_length() - 2
    chips = 1 << levels
    rows, width = rot_hbm.shape
    own = base.shape[0]
    part = own // PIECES
    items = 2 * PIECES
    me, z = lax.axis_index("row"), lax.axis_index("col")
    core, chip = lax.rem(me, 2), me // 2
    other = me + 1 - 2 * core

    def chip_bit(b):
        return (chip // (1 << b)) % 2

    def partner(b):
        return me + (2 << b) * (1 - 2 * chip_bit(b))

    def chunk(u):
        return sum((1 << b) * ((chip_bit(b) + (u >> b)) % 2) for b in range(levels))

    def remote(src, dst, send, recv, **where):
        return pltpu.make_async_remote_copy(
            src_ref=src, dst_ref=dst, send_sem=send, recv_sem=recv, device_id=where, device_id_type=MESH
        )

    barrier = pltpu.get_barrier_semaphore()
    for d in range(1, n_row):
        pl.semaphore_signal(barrier, inc=1, device_id={"row": (me + d) % n_row}, device_id_type=MESH)

    @pl.when(z > 0)
    def _():
        pl.semaphore_signal(barrier, inc=1, device_id={"col": z - 1}, device_id_type=MESH)

    @pl.when(z < n_col - 1)
    def _():
        pl.semaphore_signal(barrier, inc=1, device_id={"col": z + 1}, device_id_type=MESH)

    pl.semaphore_wait(barrier, n_row - 1 + (z + n_col - 1) // n_col + (2 * n_col - 2 - z) // n_col)

    mine = pl.ds(pl.multiple_of(core * rows, rows), rows)
    theirs = pl.ds(pl.multiple_of((1 - core) * rows, rows), rows)
    my_cols = pl.ds(pl.multiple_of(core * own, own), own)
    their_cols = pl.ds(pl.multiple_of((1 - core) * own, own), own)

    pushes = [
        remote(cols_hbm.at[their_cols], base.at[:, mine], core_send.at[0], core_recv.at[0], row=other),
        remote(rot_hbm, rot.at[mine], core_send.at[1], core_recv.at[1], row=other),
        remote(grad_hbm, grad.at[mine], core_send.at[2], core_recv.at[2], row=other),
    ]
    loads = [
        pltpu.make_async_copy(cols_hbm.at[my_cols], base.at[:, mine], load_sem.at[0]),
        pltpu.make_async_copy(rot_hbm, rot.at[mine], load_sem.at[1]),
        pltpu.make_async_copy(grad_hbm, grad.at[mine], load_sem.at[2]),
    ]
    for push, load in zip(pushes, loads):
        push.start()
        load.start()

    def order(w):
        return list(range(levels)) if w == 0 else list(range(levels - 1, -1, -1))

    def rs_messages(w):
        found = []
        for j, b in enumerate(order(w)):
            before = sum(1 << c for c in order(w)[:j])
            labels = [u for u in range(1, chips) if u & (1 << b) and not u & before]
            if j + 1 < levels:
                nxt = 1 << order(w)[j + 1]
                labels.sort(key=lambda u: 0 if u & nxt else 1)
            found.append((b, labels))
        return found

    def rs_copy(m, w, b, u):
        slot = m % 3
        return remote(
            zp.at[slot, w, chunk(u)], rbuf.at[slot, w, u - 1],
            rs_send.at[slot, w, u], rs_recv.at[slot, w, u], row=partner(b),
        )

    def ag_copy(m, w, b, u):
        slot = m % 3
        return remote(
            zf.at[slot, w, chunk(u - (1 << b))], zf.at[slot, w, chunk(u - (1 << b))],
            ag_send.at[slot, w, u], ag_recv.at[slot, w, u], row=partner(b),
        )

    def ag_labels(w, j):
        b = order(w)[j]
        later = sum(1 << c for c in order(w)[j + 1 :])
        return [u for u in range(1, chips) if u & (1 << b) and not (u - (1 << b)) & ~later]

    def add_received(m, w, b, u, final=False):
        slot = m % 3
        q = chunk(u - (1 << b))
        total = zp[slot, w, q].astype(jnp.float32) + rbuf[slot, w, u - 1].astype(jnp.float32)
        if final:
            zf[slot, w, q] = total.astype(jnp.bfloat16)
        else:
            zp[slot, w, q] = total.astype(jnp.bfloat16)

    def z_dots(m):
        slot = m % 3
        vm = m % (2 * PIECES)

        def tile(j, carry):
            at = pl.ds(pl.multiple_of(j * TILE, TILE), TILE)
            panel = v[vm].reshape(n_col * part, 2 * rows)
            for w, ref in ((0, rot), (1, grad)):
                r = jnp.dot(panel, ref[:, at], preferred_element_type=jnp.float32)
                zp[slot, w, :, :, at] = r.astype(jnp.bfloat16).reshape(chips, n_col * part // chips, TILE)
            return carry

        lax.fori_loop(0, width // TILE, tile, 0)

    def y_dots(m):
        slot = m % 3

        def tile(j, carry):
            at = pl.ds(pl.multiple_of(j * TILE, TILE), TILE)
            z1 = zf[slot, 0].reshape(n_col * part, width)
            z2 = zf[slot, 1].reshape(n_col * part, width)
            r = lax.dot_general(z1, grad[at, :], NT, preferred_element_type=jnp.float32)
            r = r - lax.dot_general(z2, rot[at, :], NT, preferred_element_type=jnp.float32)
            y[:, :, at] = r.reshape(n_col, part, TILE)
            return carry

        lax.fori_loop(0, 2 * rows // TILE, tile, 0)

    def first_sends(m):
        for j in range(1):
            for w in range(2):
                b, labels = rs_messages(w)[0]
                for u in labels:
                    rs_copy(m, w, b, u).start()

    def middle_levels(m):
        for j in range(levels - 1):
            for w in range(2):
                b, labels = rs_messages(w)[j]
                nb, nlabels = rs_messages(w)[j + 1]
                for u in labels:
                    rs_copy(m, w, b, u).wait_recv()
                    add_received(m, w, b, u)
                    if u - (1 << b) in nlabels:
                        rs_copy(m, w, nb, u - (1 << b)).start()

    def last_level(m):
        for w in range(2):
            b, labels = rs_messages(w)[levels - 1]
            for u in labels:
                rs_copy(m, w, b, u).wait_recv()
                add_received(m, w, b, u, final=True)
            for j in range(levels - 1, -1, -1):
                ag_copy(m, w, order(w)[j], 1 << order(w)[j]).start()

    def forwards(m):
        for j in range(levels - 1, 0, -1):
            for w in range(2):
                for u in ag_labels(w, j):
                    ag_copy(m, w, order(w)[j], u).wait_recv()
                    for i in range(j - 1, -1, -1):
                        b = order(w)[i]
                        ag_copy(m, w, b, u + (1 << b)).start()

    def finish_sums(m):
        for w in range(2):
            for u in ag_labels(w, 0):
                ag_copy(m, w, order(w)[0], u).wait_recv()

    def drain_sums(m):
        for w in range(2):
            for b, labels in rs_messages(w):
                for u in labels:
                    rs_copy(m, w, b, u).wait_send()
            for j in range(levels):
                for u in ag_labels(w, j):
                    ag_copy(m, w, order(w)[j], u).wait_send()

    def up_copy(m, t, way):
        slot = m % 2
        return remote(
            zsend.at[t - 1, way], zrecv.at[slot, t - 1, way],
            up_send.at[slot, t - 1, way], up_recv.at[slot, t - 1, way],
            col=jnp.clip(z + 1 - 2 * way, 0, n_col - 1),
        )

    def line_sends(m, t):
        for way in (UP, DOWN):
            far = z if way == UP else n_col - 1 - z
            dest = n_col - t + z if way == UP else t - n_col + z

            @pl.when(far + 1 <= t)
            def _(way=way, far=far, dest=dest):
                if t == 1:
                    zsend[t - 1, way] = y[dest].astype(jnp.bfloat16)
                else:

                    @pl.when(far == 0)
                    def _():
                        zsend[t - 1, way] = y[dest].astype(jnp.bfloat16)

                    @pl.when(far > 0)
                    def _():
                        up_copy(m, t - 1, way).wait_recv()
                        got = zrecv[m % 2, t - 2, way].astype(jnp.float32)
                        zsend[t - 1, way] = (y[dest] + got).astype(jnp.bfloat16)

                up_copy(m, t, way).start()

    def line_finish(m):
        t = n_col - 1
        for way in (UP, DOWN):
            far = z if way == UP else n_col - 1 - z

            @pl.when(far > 0)
            def _(way=way):
                up_copy(m, t, way).wait_recv()
                y[z] = y[z] + zrecv[m % 2, t - 1, way].astype(jnp.float32)

        for s in range(1, n_col):
            for way in (UP, DOWN):
                far = z if way == UP else n_col - 1 - z

                @pl.when(far + 1 <= s)
                def _(s=s, way=way):
                    up_copy(m, s, way).wait_send()

    def gather_copy(m, t, way):
        slot = m % 2
        block = jnp.clip(z - t + 1 if way == UP else z + t - 1, 0, n_col - 1)
        return remote(
            v.at[m, block], v.at[m, block],
            vg_send.at[slot, t - 1, way], vg_recv.at[slot, t - 1, way],
            col=jnp.clip(z + 1 - 2 * way, 0, n_col - 1),
        )

    def gather_sends(m, t):
        for way in (UP, DOWN):
            far = z if way == UP else n_col - 1 - z

            @pl.when(jnp.logical_and(far - t + 1 >= 0, far < n_col - 1))
            def _(way=way):
                gather_copy(m, t, way).start()

    def gather_waits(m, t):
        for way in (UP, DOWN):
            far = z if way == UP else n_col - 1 - z

            @pl.when(far - t >= 0)
            def _(way=way):
                gather_copy(m, t, way).wait_recv()

    def gather_drain(m):
        for t in range(1, n_col):
            for way in (UP, DOWN):
                far = z if way == UP else n_col - 1 - z

                @pl.when(jnp.logical_and(far - t + 1 >= 0, far < n_col - 1))
                def _(t=t, way=way):
                    gather_copy(m, t, way).wait_send()

    def fin_copy(p):
        at = pl.ds(p * part, part) if isinstance(p, int) else pl.ds(pl.multiple_of(p * part, part), part)
        to = pl.ds(pl.multiple_of(core * own + p * part, part), part)
        return remote(upd.at[at, theirs], fin.at[to], fin_send.at[p], fin_recv.at[p], row=other)

    hops = split(list(range(2, n_col)), 2)

    pushes[0].wait_recv()
    loads[0].wait()
    for p in range(PIECES):
        v[p, z] = base[p * part : (p + 1) * part, :]
    for t in range(1, n_col):
        gather_sends(0, t)
        gather_waits(0, t)
    gather_drain(0)
    for i in (1, 2):
        pushes[i].wait_recv()
        loads[i].wait()

    def period(it, carry):
        n = it - 2
        head, tail = n + 2 < items, jnp.logical_and(n >= 0, n < items)
        middle = jnp.logical_and(n + 1 >= 0, n + 1 < items)
        gathering = n - 1 + PIECES < items
        g = jnp.minimum(n - 1 + PIECES, items - 1)
        new = jnp.minimum(n + 2, items - 1)
        mid = jnp.clip(n + 1, 0, items - 1)
        old = jnp.clip(n, 0, items - 1)
        done = jnp.clip(n - 1, 0, items - 1)

        @pl.when(head)
        def _():
            z_dots(new)
            first_sends(new)

        @pl.when(n >= 1)
        def _():
            line_finish(done)
            p = lax.rem(done, PIECES)
            at = pl.ds(pl.multiple_of(p * part, part), part)
            panel = base[at, :].astype(jnp.float32)

            @pl.when(done < PIECES)
            def _():
                first = panel + 0.25 * y[z]
                v[g, z] = (panel + first).astype(jnp.bfloat16)

            @pl.when(done >= PIECES)
            def _():
                upd[at, :] = panel + 0.125 * y[z]
                fin_copy(p).start()

        @pl.when(gathering)
        def _():
            gather_sends(g, 1)

        @pl.when(tail)
        def _():
            finish_sums(old)
            y_dots(old)
            line_sends(old, 1)
            drain_sums(old)

        @pl.when(middle)
        def _():
            last_level(mid)

        @pl.when(gathering)
        def _():
            for t in hops[0]:
                gather_waits(g, t - 1)
                gather_sends(g, t)

        @pl.when(head)
        def _():
            middle_levels(new)

        @pl.when(gathering)
        def _():
            for t in hops[1]:
                gather_waits(g, t - 1)
                gather_sends(g, t)

        @pl.when(tail)
        def _():
            for t in hops[0]:
                line_sends(old, t)

        @pl.when(middle)
        def _():
            forwards(mid)

        @pl.when(gathering)
        def _():
            gather_waits(g, n_col - 1)
            gather_drain(g)

        @pl.when(tail)
        def _():
            for t in hops[1]:
                line_sends(old, t)

        return carry

    lax.fori_loop(0, items + 3, period, 0)

    fin[my_cols, :] = upd[:, mine]
    for p in range(PIECES):
        fin_copy(p).wait_recv()
    for p in range(PIECES):
        fin_copy(p).wait_send()
    for push in pushes:
        push.wait_send()
    result = fin[...]
    out_ref[...] = result
    ones = jnp.ones((8, rows), jnp.float32)
    nrm[...] = lax.dot_general(
        ones, result * result, NT, precision=lax.Precision.HIGHEST, preferred_element_type=jnp.float32
    )
    shares = [
        remote(nrm, nrecv.at[d - 1], n_send.at[d - 1], n_recv.at[d - 1], row=(me + d) % n_row)
        for d in range(1, n_row)
    ]
    for share in shares:
        share.start()
    total = nrm[...]
    for d, share in enumerate(shares, 1):
        share.wait_recv()
        total = total + nrecv[d - 1]
    norm_ref[...] = jnp.sqrt(total)
    for share in shares:
        share.wait_send()


def on_device(n_row, n_col, slab, rotation, gradient):
    rows, width = rotation.shape
    stride = width * n_col // slab
    own = width // stride // 2
    part = own // PIECES
    chips = n_row // 2
    k = lax.broadcasted_iota(jnp.int32, (2 * own, width), 1)
    j = lax.broadcasted_iota(jnp.int32, (2 * own, width), 0)
    pick = (k == stride * j).astype(jnp.bfloat16)
    columns = lax.dot_general(pick, rotation, NT, preferred_element_type=jnp.float32).astype(jnp.bfloat16)
    bf16, f32 = jnp.bfloat16, jnp.float32
    vmem, dma = pltpu.VMEM, pltpu.SemaphoreType.DMA
    cut = n_col * part // chips
    hop = n_col - 1
    flops = 16 * 2 * rows * width * n_col * own
    updated, norms = pl.pallas_call(
        functools.partial(kernel, n_row, n_col),
        out_shape=(
            jax.ShapeDtypeStruct((2 * own, rows), f32),
            jax.ShapeDtypeStruct((8, 2 * own), f32),
        ),
        in_specs=[pl.BlockSpec(memory_space=pl.ANY)] * 3,
        out_specs=[pl.BlockSpec(memory_space=vmem)] * 2,
        scratch_shapes=[
            vmem((2 * rows, width), bf16),
            vmem((2 * rows, width), bf16),
            vmem((own, 2 * rows), bf16),
            vmem((2 * PIECES, n_col, part, 2 * rows), bf16),
            vmem((3, 2, chips, cut, width), bf16),
            vmem((3, 2, chips, cut, width), bf16),
            vmem((3, 2, chips - 1, cut, width), bf16),
            vmem((n_col, part, 2 * rows), f32),
            vmem((hop, 2, part, 2 * rows), bf16),
            vmem((2, hop, 2, part, 2 * rows), bf16),
            vmem((own, 2 * rows), f32),
            vmem((2 * own, rows), f32),
            vmem((8, 2 * own), f32),
            vmem((n_row - 1, 8, 2 * own), f32),
            dma((3,)),
            dma((3,)),
            dma((3,)),
            dma((3, 2, chips)),
            dma((3, 2, chips)),
            dma((3, 2, chips)),
            dma((3, 2, chips)),
            dma((2, hop, 2)),
            dma((2, hop, 2)),
            dma((2, hop, 2)),
            dma((2, hop, 2)),
            dma((PIECES,)),
            dma((PIECES,)),
            dma((n_row - 1,)),
            dma((n_row - 1,)),
            dma((1,)),
        ],
        compiler_params=pltpu.CompilerParams(
            collective_id=0, has_side_effects=True, vmem_limit_bytes=67_043_328
        ),
        cost_estimate=pl.CostEstimate(flops=flops, bytes_accessed=8 * rows * width, transcendentals=0),
        name="cayley",
    )(rotation, gradient, columns)
    return updated.T, norms[0]


def solution(mesh, slab=SLAB):
    n_row, n_col = mesh.shape["row"], mesh.shape["col"]
    return jax.shard_map(
        functools.partial(on_device, n_row, n_col, slab),
        mesh=mesh,
        in_specs=(P("row", "col"), P("row", "col")),
        out_specs=(P("row", "col"), P("col")),
        check_vma=False,
    )
```

profile of v0, /device:TPU:0, one launch (start us, length us, event | category | flops | bytes accessed | tf_op | source)
XLA Modules:
  0.0 363.4 jit_solution(13605597264730564161)
XLA Ops:
  0.6 5.5 %fusion.2.cols_hbm = bf16[512,1024]{1,0:T(8,128)(2,1)} fusion(bf16[1024,2048]{1,0:T(8,128)(2,1)} %rot_hbm.1, s32[512]{0:T(512)S(1)} %iota_multiply_fusion), kind=kOutput, calls=%fused_computation.3 | convolution fusion | flops 2149056512 | bytes 5244928 | tf_op jit(solution)/shard_map/dot_general | solution.py:434
  6.2 353.0 %cayley.1 = (f32[512,1024]{1,0:T(8,128)}, f32[8,512]{1,0:T(8,128)}) custom-call(bf16[1024,2048]{1,0:T(8,128)(2,1)} %rot_hbm.1, bf16[1024,2048]{1,0:T(8,128)(2,1)} %grad_hbm.1, bf16[512,1024]{1,0:T(8,128)(2,1)} %fusion.2.cols_hbm), custom_call_target="tpu_custom_call" | custom-call | flops 68719476736 | bytes 16777216 | tf_op jit(solution)/shard_map/cayley/pallas_call | solution.py:440
  359.2 2.9 copy.4
  362.1 1.3 slice.3
  (1 shorter events, 0.0 us)
where the time goes:
time: 364 us; the launch traced here: 363 us
  Pallas kernels  353 us (97%)
  matrix products  5.54 us (2%)
  local copies, waits for them, and re-layouts  4.18 us (1%)
    pallas_call x1, Pallas kernels, on_device(): pl.pallas_call(functools.partial(kernel, n_row, n_col), out_shape=(jax.Sh...  353 us

commit v1 on v0

v1 whole, which is shorter than its diff:
```python
import functools

import jax
import jax.numpy as jnp
from jax import lax
from jax.experimental import pallas as pl
from jax.experimental.pallas import tpu as pltpu
from jax.sharding import PartitionSpec as P

SLAB = 2048
PIECES = 4
TILE = 256
LANES = 128
MESH = pl.DeviceIdType.MESH
NT = (((1,), (1,)), ((), ()))
UP, DOWN = 0, 1


def split(items, groups):
    size = -(-len(items) // groups)
    return [items[g * size : (g + 1) * size] for g in range(groups)]


def kernel(
    n_row, n_col, stride,
    rot_hbm, grad_hbm,
    out_hbm, norm_ref,
    rot, grad, picked, base, v, zp, zf, rbuf, y, acc, zsend, zrecv, fin, sq, nrm, nrecv,
    load_sem, core_send, core_recv, rs_send, rs_recv, ag_send, ag_recv,
    up_send, up_recv, vg_send, vg_recv, n_send, n_recv,
):
    levels = n_row.bit_length() - 2
    chips = 1 << levels
    rows, width = rot_hbm.shape
    own = base.shape[0]
    part = own // PIECES
    last = 2 * PIECES + 1
    rest = (n_col - 1) * part
    depth = width // chips
    z_tile = min(TILE, depth)
    per_chunk = depth // z_tile
    me, z = lax.axis_index("row"), lax.axis_index("col")
    core, chip = lax.rem(me, 2), me // 2
    other = me + 1 - 2 * core

    def chip_bit(b):
        return (chip // (1 << b)) % 2

    def partner(b):
        return me + (2 << b) * (1 - 2 * chip_bit(b))

    def chunk(u):
        return sum((1 << b) * ((chip_bit(b) + (u >> b)) % 2) for b in range(levels))

    def remote(src, dst, send, recv, **where):
        return pltpu.make_async_remote_copy(
            src_ref=src, dst_ref=dst, send_sem=send, recv_sem=recv, device_id=where, device_id_type=MESH
        )

    mine = pl.ds(pl.multiple_of(core * rows, rows), rows)
    theirs = pl.ds(pl.multiple_of((1 - core) * rows, rows), rows)
    my_cols = pl.ds(pl.multiple_of(core * own, own), own)
    their_cols = pl.ds(pl.multiple_of((1 - core) * own, own), own)

    loads = [
        pltpu.make_async_copy(rot_hbm, rot.at[mine], load_sem.at[0]),
        pltpu.make_async_copy(grad_hbm, grad.at[mine], load_sem.at[1]),
    ]
    for load in loads:
        load.start()

    barrier = pltpu.get_barrier_semaphore()
    for d in range(1, n_row):
        pl.semaphore_signal(barrier, inc=1, device_id={"row": (me + d) % n_row}, device_id_type=MESH)

    @pl.when(z > 0)
    def _():
        pl.semaphore_signal(barrier, inc=1, device_id={"col": z - 1}, device_id_type=MESH)

    @pl.when(z < n_col - 1)
    def _():
        pl.semaphore_signal(barrier, inc=1, device_id={"col": z + 1}, device_id_type=MESH)

    pl.semaphore_wait(barrier, n_row - 1 + (z + n_col - 1) // n_col + (2 * n_col - 2 - z) // n_col)

    def push(w, u):
        at = pl.ds(pl.multiple_of(chunk(u) * depth, depth), depth)
        src, dst = ((rot_hbm, rot), (grad_hbm, grad))[w]
        return remote(src.at[:, at], dst.at[mine, at], core_send.at[w, u], core_recv.at[w, u], row=other)

    chunk_order = list(range(chips - 1, -1, -1))
    for u in chunk_order:
        for w in range(2):
            push(w, u).start()

    def order(w):
        return list(range(levels)) if w == 0 else list(range(levels - 1, -1, -1))

    def rs_messages(w):
        found = []
        for j, b in enumerate(order(w)):
            before = sum(1 << c for c in order(w)[:j])
            labels = [u for u in range(1, chips) if u & (1 << b) and not u & before]
            if j + 1 < levels:
                nxt = 1 << order(w)[j + 1]
                labels.sort(key=lambda u: 0 if u & nxt else 1)
            found.append((b, labels))
        return found

    def rs_copy(m, height, w, b, u):
        slot, at = m % 3, pl.ds(0, height)
        return remote(
            zp.at[slot, w, chunk(u), at], rbuf.at[slot, w, u - 1, at],
            rs_send.at[slot, w, u], rs_recv.at[slot, w, u], row=partner(b),
        )

    def ag_copy(m, height, w, b, u):
        slot, at = m % 3, pl.ds(0, height)
        ref = zf.at[slot, w, chunk(u - (1 << b)), at]
        return remote(ref, ref, ag_send.at[slot, w, u], ag_recv.at[slot, w, u], row=partner(b))

    def ag_labels(w, j):
        b = order(w)[j]
        later = sum(1 << c for c in order(w)[j + 1 :])
        return [u for u in range(1, chips) if u & (1 << b) and not (u - (1 << b)) & ~later]

    def add_received(m, height, w, b, u, ref):
        slot, at = m % 3, pl.ds(0, height)
        q = chunk(u - (1 << b))
        total = zp[slot, w, q, at, :].astype(jnp.float32) + rbuf[slot, w, u - 1, at, :].astype(jnp.float32)
        ref[slot, w, q, at, :] = total.astype(jnp.bfloat16)

    def z_tile_dot(slot, w, panel, j):
        at = pl.ds(pl.multiple_of(j * z_tile, z_tile), z_tile)
        to = pl.ds(pl.multiple_of((j % per_chunk) * z_tile, z_tile), z_tile)
        r = jnp.dot(panel, (rot, grad)[w][:, at], preferred_element_type=jnp.float32)
        zp[slot, w, j // per_chunk, pl.ds(0, panel.shape[0]), to] = r.astype(jnp.bfloat16)

    def z_dots(m, panel_of):
        def tile(j, carry):
            panel = panel_of()
            for w in range(2):
                z_tile_dot(m % 3, w, panel, j)
            return carry

        lax.fori_loop(0, width // z_tile, tile, 0)

    def rest_panel(g):
        return jnp.concatenate([v[g, (z + d) % n_col] for d in range(1, n_col)], axis=0)

    def own_panel():
        return jnp.concatenate([v[PIECES + p, z] for p in range(PIECES)], axis=0)

    def y_tile_dot(m, height, at):
        z1, z2 = (
            jnp.concatenate([zf[m % 3, w, q, pl.ds(0, height), :] for q in range(chips)], axis=1)
            for w in range(2)
        )
        r = lax.dot_general(z1, grad[at, :], NT, preferred_element_type=jnp.float32)
        return r - lax.dot_general(z2, rot[at, :], NT, preferred_element_type=jnp.float32)

    y_tiles = 2 * rows // TILE

    def y_rest(m):
        def tile(j, carry):
            at = pl.ds(pl.multiple_of(j * TILE, TILE), TILE)
            r = y_tile_dot(m, rest, at)
            for d in range(1, n_col):
                y[m % 2, (z + d) % n_col, :, at] = r[(d - 1) * part : d * part]
            return carry

        lax.fori_loop(0, y_tiles, tile, 0)

    def y_first():
        def tile(j, carry):
            at = pl.ds(pl.multiple_of(j * TILE, TILE), TILE)
            acc[:, at] = y_tile_dot(0, own, at)
            return carry

        lax.fori_loop(0, y_tiles, tile, 0)

    def first_sends(m, height):
        for w in range(2):
            b, labels = rs_messages(w)[0]
            for u in labels:
                rs_copy(m, height, w, b, u).start()

    def middle_levels(m, height):
        for j in range(levels - 1):
            for w in range(2):
                b, labels = rs_messages(w)[j]
                nb, nlabels = rs_messages(w)[j + 1]
                for u in labels:
                    rs_copy(m, height, w, b, u).wait_recv()
                    add_received(m, height, w, b, u, zp)
                    if u - (1 << b) in nlabels:
                        rs_copy(m, height, w, nb, u - (1 << b)).start()

    def last_level(m, height):
        for w in range(2):
            b, labels = rs_messages(w)[levels - 1]
            for u in labels:
                rs_copy(m, height, w, b, u).wait_recv()
                add_received(m, height, w, b, u, zf)
            for j in range(levels - 1, -1, -1):
                ag_copy(m, height, w, order(w)[j], 1 << order(w)[j]).start()

    def forwards(m, height):
        for j in range(levels - 1, 0, -1):
            for w in range(2):
                for u in ag_labels(w, j):
                    ag_copy(m, height, w, order(w)[j], u).wait_recv()
                    for i in range(j - 1, -1, -1):
                        b = order(w)[i]
                        ag_copy(m, height, w, b, u + (1 << b)).start()

    def finish_sums(m, height):
        for w in range(2):
            for u in ag_labels(w, 0):
                ag_copy(m, height, w, order(w)[0], u).wait_recv()

    def drain_sums(m, height):
        for w in range(2):
            for b, labels in rs_messages(w):
                for u in labels:
                    rs_copy(m, height, w, b, u).wait_send()
            for j in range(levels):
                for u in ag_labels(w, j):
                    ag_copy(m, height, w, order(w)[j], u).wait_send()

    def line_copy(m, t, way):
        return remote(
            zsend.at[m % 2, t - 1, way], zrecv.at[m % 3, t - 1, way],
            up_send.at[m % 2, t - 1, way], up_recv.at[m % 3, t - 1, way],
            col=jnp.clip(z + 1 - 2 * way, 0, n_col - 1),
        )

    def line_sends(m, t):
        slot = m % 2
        for way in (UP, DOWN):
            far = z if way == UP else n_col - 1 - z
            dest = n_col - t + z if way == UP else t - n_col + z

            @pl.when(far + 1 <= t)
            def _(way=way, far=far, dest=dest):
                @pl.when(far == 0)
                def _():
                    zsend[slot, t - 1, way] = y[slot, dest].astype(jnp.bfloat16)

                if t > 1:

                    @pl.when(far > 0)
                    def _():
                        line_copy(m, t - 1, way).wait_recv()
                        got = zrecv[m % 3, t - 2, way].astype(jnp.float32)
                        zsend[slot, t - 1, way] = (y[slot, dest] + got).astype(jnp.bfloat16)

                line_copy(m, t, way).start()

    def line_finish(m, p, total, put):
        t = n_col - 1
        for way in (UP, DOWN):
            far = z if way == UP else n_col - 1 - z

            @pl.when(far > 0)
            def _(way=way):
                line_copy(m, t, way).wait_recv()

        at = pl.ds(pl.multiple_of(p * part, part), part)
        panel = base[at, :].astype(jnp.float32)

        @pl.when(z == 0)
        def _():
            put(at, panel, total(at) + zrecv[m % 3, t - 1, DOWN].astype(jnp.float32))

        @pl.when(z == n_col - 1)
        def _():
            put(at, panel, total(at) + zrecv[m % 3, t - 1, UP].astype(jnp.float32))

        @pl.when(jnp.logical_and(z > 0, z < n_col - 1))
        def _():
            got = zrecv[m % 3, t - 1, UP].astype(jnp.float32) + zrecv[m % 3, t - 1, DOWN].astype(jnp.float32)
            put(at, panel, total(at) + got)

    def line_drain(m):
        for s in range(1, n_col):
            for way in (UP, DOWN):
                far = z if way == UP else n_col - 1 - z

                @pl.when(far + 1 <= s)
                def _(s=s, way=way):
                    line_copy(m, s, way).wait_send()

    def to_middle(m):
        p = (m - 1) % PIECES

        def put(at, panel, total):
            first = panel + 0.25 * total
            v[PIECES + p, z] = (panel + first).astype(jnp.bfloat16)

        line_finish(m, p, lambda at: acc[at, :], put)
        line_drain(m)

    def to_updated(m):
        def put(at, panel, total):
            acc[at, :] = panel + 0.125 * total

        line_finish(m, (m - 1) % PIECES, lambda at: 0.0, put)
        line_drain(m)

    def gather_copy(g, t, way):
        slot = g % 2
        block = jnp.clip(z - t + 1 if way == UP else z + t - 1, 0, n_col - 1)
        return remote(
            v.at[g, block], v.at[g, block],
            vg_send.at[slot, t - 1, way], vg_recv.at[slot, t - 1, way],
            col=jnp.clip(z + 1 - 2 * way, 0, n_col - 1),
        )

    def gather_sends(g, t):
        for way in (UP, DOWN):
            far = z if way == UP else n_col - 1 - z

            @pl.when(jnp.logical_and(far - t + 1 >= 0, far < n_col - 1))
            def _(way=way):
                gather_copy(g, t, way).start()

    def gather_waits(g, t):
        for way in (UP, DOWN):
            far = z if way == UP else n_col - 1 - z

            @pl.when(far - t >= 0)
            def _(way=way):
                gather_copy(g, t, way).wait_recv()

    def gather_drain(g):
        for t in range(1, n_col):
            for way in (UP, DOWN):
                far = z if way == UP else n_col - 1 - z

                @pl.when(jnp.logical_and(far - t + 1 >= 0, far < n_col - 1))
                def _(t=t, way=way):
                    gather_copy(g, t, way).wait_send()

    hops = split(list(range(2, n_col)), 2)

    def gather_hops(g, group):
        for t in hops[group]:
            gather_waits(g, t - 1)
            gather_sends(g, t)

    def line_hops(m, group):
        for t in hops[group]:
            line_sends(m, t)

    loads[0].wait()
    few = TILE // stride
    pick = (
        lax.broadcasted_iota(jnp.int32, (few, TILE), 1) == stride * lax.broadcasted_iota(jnp.int32, (few, TILE), 0)
    ).astype(jnp.bfloat16)

    def pick_tile(j, carry):
        at = pl.ds(pl.multiple_of(j * TILE, TILE), TILE)
        r = lax.dot_general(pick, rot[mine, at], NT, preferred_element_type=jnp.float32)
        picked[pl.ds(pl.multiple_of(j * few, few), few), :] = r.astype(jnp.bfloat16)
        return carry

    lax.fori_loop(0, width // TILE, pick_tile, 0)
    base_push = remote(
        picked.at[their_cols], base.at[:, mine], core_send.at[2, 0], core_recv.at[2, 0], row=other
    )
    base_push.start()
    base[:, mine] = picked[my_cols, :]
    base_push.wait_recv()
    for p in range(PIECES):
        v[p, z] = base[p * part : (p + 1) * part, :]
    gather_sends(0, 1)

    loads[1].wait()
    for u in chunk_order:
        for w in range(2):
            push(w, u).wait_recv()

        def tile(j, carry, u=u):
            panel = base[...]
            for w in range(2):
                z_tile_dot(0, w, panel, chunk(u) * per_chunk + j)
            return carry

        lax.fori_loop(0, per_chunk, tile, 0)
        for w in range(2):
            b, labels = rs_messages(w)[0]
            if u in labels:
                rs_copy(0, own, w, b, u).start()

    gather_hops(0, 0)
    middle_levels(0, own)
    gather_hops(0, 1)
    last_level(0, own)
    gather_waits(0, n_col - 1)
    gather_drain(0)

    def period(it, carry):
        n = it - 1
        gathering = n + 2 < 2 * PIECES
        g = jnp.minimum(n + 2, 2 * PIECES - 1)
        new, mid, old = n + 2, n + 1, jnp.maximum(n, 0)
        done = jnp.maximum(n - 1, 1)

        z_dots(new, lambda: rest_panel(new - 1))
        first_sends(new, rest)

        @pl.when(jnp.logical_and(n >= 2, n - 1 <= PIECES))
        def _():
            to_middle(done)

        @pl.when(n - 1 > PIECES)
        def _():
            to_updated(done)

        @pl.when(gathering)
        def _():
            gather_sends(g, 1)

        @pl.when(n == 0)
        def _():
            finish_sums(0, own)
            y_first()
            drain_sums(0, own)

        @pl.when(n >= 1)
        def _():
            finish_sums(old, rest)
            y_rest(old)
            line_sends(old, 1)
            drain_sums(old, rest)

        @pl.when(n >= 0)
        def _():
            last_level(mid, rest)

        @pl.when(gathering)
        def _():
            gather_hops(g, 0)

        middle_levels(new, rest)

        @pl.when(gathering)
        def _():
            gather_hops(g, 1)

        @pl.when(n >= 1)
        def _():
            line_hops(old, 0)

        @pl.when(n == -1)
        def _():
            forwards(0, own)

        @pl.when(n >= 0)
        def _():
            forwards(mid, rest)

        @pl.when(gathering)
        def _():
            gather_waits(g, n_col - 1)
            gather_drain(g)

        @pl.when(n >= 1)
        def _():
            line_hops(old, 1)

        return carry

    lax.fori_loop(0, last - 1, period, 0)

    last_level(last - 1, rest)
    z_dots(last, own_panel)
    forwards(last - 1, rest)
    first_sends(last, own)
    to_updated(last - 3)
    finish_sums(last - 2, rest)
    y_rest(last - 2)
    line_sends(last - 2, 1)
    middle_levels(last, own)
    line_hops(last - 2, 0)
    finish_sums(last - 1, rest)
    y_rest(last - 1)
    line_sends(last - 1, 1)
    last_level(last, own)
    line_hops(last - 2, 1)
    line_hops(last - 1, 0)
    forwards(last, own)
    to_updated(last - 2)
    line_hops(last - 1, 1)
    drain_sums(last - 2, rest)
    drain_sums(last - 1, rest)
    to_updated(last - 1)
    finish_sums(last, own)

    sq[...] = jnp.zeros_like(sq)
    fin_push = remote(acc.at[:, theirs], fin, core_send.at[2, 1], core_recv.at[2, 1], row=other)

    def final_tile(j, carry):
        i = (j + (1 - core) * (y_tiles // 2)) % y_tiles
        at = pl.ds(pl.multiple_of(i * TILE, TILE), TILE)
        result = acc[:, at] + 0.125 * y_tile_dot(last, own, at)
        acc[:, at] = result
        squares = result * result
        sq[...] += sum(squares[:, k : k + LANES] for k in range(0, TILE, LANES))

        @pl.when(j == y_tiles // 2 - 1)
        def _():
            fin_push.start()

        return carry

    lax.fori_loop(0, y_tiles, final_tile, 0)
    keep = pltpu.make_async_copy(acc.at[:, mine], out_hbm.at[my_cols], load_sem.at[0])
    keep.start()
    nrm[...] = lax.dot_general(
        jnp.ones((8, LANES), jnp.float32), sq[...], NT,
        precision=lax.Precision.HIGHEST, preferred_element_type=jnp.float32,
    )
    shares = [
        remote(nrm, nrecv.at[d - 1], n_send.at[d - 1], n_recv.at[d - 1], row=(me + d) % n_row)
        for d in range(1, n_row)
    ]
    for share in shares:
        share.start()
    fin_push.wait_recv()
    bring = pltpu.make_async_copy(fin, out_hbm.at[their_cols], load_sem.at[1])
    bring.start()
    totals = [nrm[...], jnp.zeros_like(nrm)]
    for d, share in enumerate(shares, 1):
        share.wait_recv()
        totals[d % 2] = totals[d % 2] + nrecv[d - 1]
    norm_ref[:, my_cols] = jnp.sqrt(totals[0])
    norm_ref[:, their_cols] = jnp.sqrt(totals[1])
    for share in shares:
        share.wait_send()
    drain_sums(last, own)
    base_push.wait_send()
    fin_push.wait_send()
    for u in chunk_order:
        for w in range(2):
            push(w, u).wait_send()
    keep.wait()
    bring.wait()


def on_device(n_row, n_col, slab, rotation, gradient):
    rows, width = rotation.shape
    stride = width * n_col // slab
    own = width // stride // 2
    part = own // PIECES
    chips = n_row // 2
    bf16, f32 = jnp.bfloat16, jnp.float32
    vmem, dma = pltpu.VMEM, pltpu.SemaphoreType.DMA
    height = max(own, (n_col - 1) * part)
    depth = width // chips
    hop = n_col - 1
    flops = 16 * 2 * rows * width * n_col * own
    updated, norms = pl.pallas_call(
        functools.partial(kernel, n_row, n_col, stride),
        out_shape=(
            jax.ShapeDtypeStruct((2 * own, rows), f32),
            jax.ShapeDtypeStruct((8, 2 * own), f32),
        ),
        in_specs=[pl.BlockSpec(memory_space=pl.ANY)] * 2,
        out_specs=[pl.BlockSpec(memory_space=pl.ANY), pl.BlockSpec(memory_space=vmem)],
        scratch_shapes=[
            vmem((2 * rows, width), bf16),
            vmem((2 * rows, width), bf16),
            vmem((2 * own, rows), bf16),
            vmem((own, 2 * rows), bf16),
            vmem((2 * PIECES, n_col, part, 2 * rows), bf16),
            vmem((3, 2, chips, height, depth), bf16),
            vmem((3, 2, chips, height, depth), bf16),
            vmem((3, 2, chips - 1, height, depth), bf16),
            vmem((2, n_col, part, 2 * rows), f32),
            vmem((own, 2 * rows), f32),
            vmem((2, hop, 2, part, 2 * rows), bf16),
            vmem((3, hop, 2, part, 2 * rows), bf16),
            vmem((own, rows), f32),
            vmem((own, LANES), f32),
            vmem((8, own), f32),
            vmem((n_row - 1, 8, own), f32),
            dma((2,)),
            dma((3, chips)),
            dma((3, chips)),
            dma((3, 2, chips)),
            dma((3, 2, chips)),
            dma((3, 2, chips)),
            dma((3, 2, chips)),
            dma((2, hop, 2)),
            dma((3, hop, 2)),
            dma((2, hop, 2)),
            dma((2, hop, 2)),
            dma((n_row - 1,)),
            dma((n_row - 1,)),
        ],
        compiler_params=pltpu.CompilerParams(
            collective_id=0, has_side_effects=True, vmem_limit_bytes=67_043_328
        ),
        cost_estimate=pl.CostEstimate(flops=flops, bytes_accessed=8 * rows * width, transcendentals=0),
        name="cayley",
    )(rotation, gradient)
    return updated.T, norms[0]


def solution(mesh, slab=SLAB):
    n_row, n_col = mesh.shape["row"], mesh.shape["col"]
    return jax.shard_map(
        functools.partial(on_device, n_row, n_col, slab),
        mesh=mesh,
        in_specs=(P("row", "col"), P("row", "col")),
        out_specs=(P("row", "col"), P("col")),
        check_vma=False,
    )
```

time: 364 us -> 331 us (0.909)
  Pallas kernels: 353 us -> 326 us
  matrix products: 5.54 us -> 0 us
    pallas_call x1, Pallas kernels: 353 us -> 326 us  [on_device(): pl.pallas_call(functools.partial(kernel, n_row, n_col, stride), out_shape...]
    dot_general x1 -> x0, matrix products: 5.54 us -> none  [on_device(): lax.dot_general(pick, rotation, NT, preferred_element_type=jnp.float32)]
where the time goes in v1:
time: 331 us
  Pallas kernels  326 us (98%)
  local copies, waits for them, and re-layouts  4.18 us (1%)
    pallas_call x1, Pallas kernels, on_device(): pl.pallas_call(functools.partial(kernel, n_row, n_col, stride), out_shape...  326 us

profile of v1, /device:TPU:0, one launch (start us, length us, event | category | flops | bytes accessed | tf_op | source)
XLA Modules:
  0.0 330.8 jit_solution(16384747407128400632)
XLA Ops:
  0.6 326.0 %cayley.1 = (f32[512,1024]{1,0:T(8,128)}, f32[8,512]{1,0:T(8,128)}) custom-call(bf16[1024,2048]{1,0:T(8,128)(2,1)} %rot_hbm.1, bf16[1024,2048]{1,0:T(8,128)(2,1)} %grad_hbm.1), custom_call_target="tpu_custom_call" | custom-call | flops 68719476736 | bytes 16777216 | tf_op jit(solution)/shard_map/cayley/pallas_call | solution.py:564
  326.6 2.9 copy.4
  329.5 1.3 slice.3

commit v2 on v1

--- a/solution.py
+++ b/solution.py
@@ -89,9 +89,8 @@
         return remote(src.at[:, at], dst.at[mine, at], core_send.at[w, u], core_recv.at[w, u], row=other)
 
     chunk_order = list(range(chips - 1, -1, -1))
-    for u in chunk_order:
-        for w in range(2):
-            push(w, u).start()
+    for w in range(2):
+        push(w, chunk_order[0]).start()
 
     def order(w):
         return list(range(levels)) if w == 0 else list(range(levels - 1, -1, -1))
@@ -202,7 +201,9 @@
             for u in labels:
                 rs_copy(m, height, w, b, u).wait_recv()
                 add_received(m, height, w, b, u, zf)
-            for j in range(levels - 1, -1, -1):
+            ag_copy(m, height, w, b, 1 << b).start()
+        for j in range(levels - 2, -1, -1):
+            for w in range(2):
                 ag_copy(m, height, w, order(w)[j], 1 << order(w)[j]).start()
 
     def forwards(m, height):
@@ -309,7 +310,7 @@
         line_drain(m)
 
     def gather_copy(g, t, way):
-        slot = g % 2
+        slot = g % PIECES
         block = jnp.clip(z - t + 1 if way == UP else z + t - 1, 0, n_col - 1)
         return remote(
             v.at[g, block], v.at[g, block],
@@ -370,6 +371,9 @@
         picked.at[their_cols], base.at[:, mine], core_send.at[2, 0], core_recv.at[2, 0], row=other
     )
     base_push.start()
+    for u in chunk_order[1:]:
+        for w in range(2):
+            push(w, u).start()
     base[:, mine] = picked[my_cols, :]
     base_push.wait_recv()
     for p in range(PIECES):
@@ -377,7 +381,7 @@
     gather_sends(0, 1)
 
     loads[1].wait()
-    for u in chunk_order:
+    for i, u in enumerate(chunk_order):
         for w in range(2):
             push(w, u).wait_recv()
 
@@ -392,83 +396,106 @@
             b, labels = rs_messages(w)[0]
             if u in labels:
                 rs_copy(0, own, w, b, u).start()
-
-    gather_hops(0, 0)
+        if i == chips - 2:
+            gather_hops(0, 0)
+
     middle_levels(0, own)
     gather_hops(0, 1)
+    for p in range(1, PIECES):
+        gather_sends(p, 1)
     last_level(0, own)
     gather_waits(0, n_col - 1)
-    gather_drain(0)
 
     def period(it, carry):
         n = it - 1
         gathering = n + 2 < 2 * PIECES
+        later = jnp.logical_and(n + 2 >= PIECES, gathering)
         g = jnp.minimum(n + 2, 2 * PIECES - 1)
-        new, mid, old = n + 2, n + 1, jnp.maximum(n, 0)
-        done = jnp.maximum(n - 1, 1)
+        new, mid, old = n + 2, jnp.maximum(n + 1, 1), jnp.maximum(n, 1)
+        behind, product = jnp.maximum(n - 1, 1), jnp.maximum(jnp.minimum(n + 1, jnp.maximum(n, PIECES)), 1)
+        follow = jnp.minimum(old + PIECES - 1, 2 * PIECES - 1)
+
+        @pl.when(n >= 0)
+        def _():
+            last_level(mid, rest)
 
         z_dots(new, lambda: rest_panel(new - 1))
+
+        @pl.when(n == -1)
+        def _():
+            forwards(0, own)
+
+        @pl.when(jnp.logical_and(n >= 0, n < PIECES))
+        def _():
+            forwards(mid, rest)
+
         first_sends(new, rest)
 
-        @pl.when(jnp.logical_and(n >= 2, n - 1 <= PIECES))
-        def _():
-            to_middle(done)
-
-        @pl.when(n - 1 > PIECES)
-        def _():
-            to_updated(done)
-
-        @pl.when(gathering)
-        def _():
-            gather_sends(g, 1)
-
-        @pl.when(n == 0)
-        def _():
+        @pl.when(jnp.logical_and(n >= 1, n <= PIECES))
+        def _():
+            line_hops(old, 0)
+
+        @pl.when(n > PIECES + 1)
+        def _():
+            line_hops(behind, 1)
+
+        @pl.when(later)
+        def _():
+            gather_hops(g, 0)
+
+        @pl.when(n == -1)
+        def _():
+            for p in range(1, PIECES):
+                gather_hops(p, 0)
+            gather_hops(1, 1)
             finish_sums(0, own)
             y_first()
             drain_sums(0, own)
 
-        @pl.when(n >= 1)
-        def _():
-            finish_sums(old, rest)
-            y_rest(old)
-            line_sends(old, 1)
-            drain_sums(old, rest)
-
-        @pl.when(n >= 0)
-        def _():
-            last_level(mid, rest)
+        @pl.when(n == 0)
+        def _():
+            for p in range(2, PIECES):
+                gather_hops(p, 1)
+
+        @pl.when(jnp.logical_and(n >= 1, n <= PIECES))
+        def _():
+            line_hops(old, 1)
+
+        @pl.when(later)
+        def _():
+            gather_hops(g, 1)
+
+        @pl.when(jnp.logical_and(n >= 0, n != PIECES))
+        def _():
+            finish_sums(product, rest)
+            y_rest(product)
+            line_sends(product, 1)
+            drain_sums(product, rest)
+
+        middle_levels(new, rest)
+
+        @pl.when(n >= PIECES)
+        def _():
+            forwards(mid, rest)
+
+        @pl.when(jnp.logical_and(n >= 1, n <= PIECES))
+        def _():
+            to_middle(old)
+            gather_sends(follow, 1)
+
+        @pl.when(n > PIECES + 1)
+        def _():
+            to_updated(behind)
+
+        @pl.when(n > PIECES)
+        def _():
+            line_hops(old, 0)
+
+        gather_drain(n + 1)
 
         @pl.when(gathering)
         def _():
-            gather_hops(g, 0)
-
-        middle_levels(new, rest)
-
-        @pl.when(gathering)
-        def _():
-            gather_hops(g, 1)
-
-        @pl.when(n >= 1)
-        def _():
-            line_hops(old, 0)
-
-        @pl.when(n == -1)
-        def _():
-            forwards(0, own)
-
-        @pl.when(n >= 0)
-        def _():
-            forwards(mid, rest)
-
-        @pl.when(gathering)
-        def _():
             gather_waits(g, n_col - 1)
-            gather_drain(g)
-
-        @pl.when(n >= 1)
-        def _():
-            line_hops(old, 1)
 
         return carry
 
@@ -478,10 +505,11 @@
     z_dots(last, own_panel)
     forwards(last - 1, rest)
     first_sends(last, own)
-    to_updated(last - 3)
+    line_hops(last - 3, 1)
     finish_sums(last - 2, rest)
     y_rest(last - 2)
     line_sends(last - 2, 1)
+    to_updated(last - 3)
     middle_levels(last, own)
     line_hops(last - 2, 0)
     finish_sums(last - 1, rest)
@@ -595,8 +623,8 @@
             dma((3, 2, chips)),
             dma((2, hop, 2)),
             dma((3, hop, 2)),
-            dma((2, hop, 2)),
-            dma((2, hop, 2)),
+            dma((PIECES, hop, 2)),
+            dma((PIECES, hop, 2)),
             dma((n_row - 1,)),
             dma((n_row - 1,)),
         ],

time: 331 us -> 328 us (level)
  no operation moved by 1% of the time
where the time goes in v2:
time: 328 us
  Pallas kernels  323 us (98%)
  local copies, waits for them, and re-layouts  4.18 us (1%)
    pallas_call x1, Pallas kernels, on_device(): pl.pallas_call(functools.partial(kernel, n_row, n_col, stride), out_shape...  323 us

profile of v2, /device:TPU:0, one launch (start us, length us, event | category | flops | bytes accessed | tf_op | source)
XLA Modules:
  0.0 328.2 jit_solution(11822145213464850266)
XLA Ops:
  0.6 323.4 %cayley.1 = (f32[512,1024]{1,0:T(8,128)}, f32[8,512]{1,0:T(8,128)}) custom-call(bf16[1024,2048]{1,0:T(8,128)(2,1)} %rot_hbm.1, bf16[1024,2048]{1,0:T(8,128)(2,1)} %grad_hbm.1), custom_call_target="tpu_custom_call" | custom-call | flops 68719476736 | bytes 16777216 | tf_op jit(solution)/shard_map/cayley/pallas_call | solution.py:592
  324.0 2.9 copy.4
  326.9 1.3 slice.3
